TPU v7x, 32 devices: a whole 2x2x4 slice. The times are simulated.
32 devices in a mesh: owner: 4 (over y, x), rows: 8 (over z, core).
Axes of the slice: x: 2, y: 2, z: 4, core: 2. Of those that a mesh axis runs over, the one named last changes fastest.
Arguments:
- w_gate: float32 [64, 2048, 1024], P('owner', 'rows'), may hold values from -0.1875 to 0.1875
- avg_gate: bfloat16 [64, 2048, 1024], P('owner', 'rows'), may hold values from -0.0625 to 0.0625
- w_up: float32 [64, 2048, 1024], P('owner', 'rows'), may hold values from -0.1875 to 0.1875
- avg_up: bfloat16 [64, 2048, 1024], P('owner', 'rows'), may hold values from -0.0625 to 0.0625
- w_down: float32 [64, 1024, 2048], P('owner', None, 'rows'), may hold values from -0.25 to 0.25
- avg_down: bfloat16 [64, 1024, 2048], P('owner', None, 'rows'), may hold values from -0.09375 to 0.09375
- router_weight: float32 [2048, 64], P('rows', 'owner'), may hold values from -0.125 to 0.125
- router_gain: float32 [2048], P('rows'), may hold values from 0.25 to 1.75
Outputs:
- serve_gate: bfloat16 [64, 2048, 1024], P('owner', None, 'rows')
- serve_up: bfloat16 [64, 2048, 1024], P('owner', None, 'rows')
- serve_down: bfloat16 [64, 1024, 2048], P('owner', 'rows')
- scale_gate: float32 [64, 1024], P('owner', 'rows')
- scale_up: float32 [64, 1024], P('owner', 'rows')
- scale_down: float32 [64, 1024], P('owner', 'rows')
- serve_router: bfloat16 [2048, 64], replicated
All inputs are finite; a program needn't handle non-finite values.
Results may differ from a plain program's by a relative error of at most 0.0015.
Values may be sent and summed in bfloat16 or wider, within the bound.
A program may use at most 192 MiB of HBM per device.

v0:
```python
import jax
import jax.numpy as jnp
from jax import lax
from jax.experimental import pallas as pl
from jax.experimental.pallas import tpu as pltpu
from jax.sharding import PartitionSpec as P

LANES = 128
STEP = 4


def columns_sum(w, a, o):
    @pl.loop(0, w.shape[0])
    def _(e):
        fresh = w[e] + a[e].astype(jnp.float32)
        o[e] = jnp.sum(fresh * fresh, axis=0, keepdims=True)


def rows_sum(w, a, o):
    @pl.loop(0, w.shape[0])
    def _(e):
        fresh = w[e] + a[e].astype(jnp.float32)
        square = fresh * fresh
        folded = square[:, :LANES]
        for start in range(LANES, square.shape[1], LANES):
            folded = folded + square[:, start : start + LANES]
        o[e] = jnp.sum(folded.T, axis=0, keepdims=True)


def columns_norm(w, a, s, *refs):
    o = refs[-1]

    @pl.loop(0, w.shape[0])
    def _(e):
        fresh = (w[e] + a[e].astype(jnp.float32)) * (1.0 / s[e])
        for part in range(o.shape[0]):
            o[part, e] = fresh[:, part * LANES : (part + 1) * LANES].astype(o.dtype)


def rows_norm(w, a, s, *refs):
    o = refs[-1]
    height = w.shape[1] // o.shape[0]

    @pl.loop(0, w.shape[0])
    def _(e):
        inverse = 1.0 / s[e]
        for part in range(o.shape[0]):
            rows = slice(part * height, (part + 1) * height)
            factor = jnp.broadcast_to(inverse[:, rows], (LANES, height)).T
            for piece in range(w.shape[2] // LANES):
                lanes = slice(piece * LANES, (piece + 1) * LANES)
                fresh = w[e, rows, lanes] + a[e, rows, lanes].astype(jnp.float32)
                o[part, e, piece * height : (piece + 1) * height, :] = (fresh * factor).astype(o.dtype)


def stack_rows(x, *refs):
    o = refs[-1]
    height = x.shape[2]

    @pl.loop(0, x.shape[1])
    def _(e):
        for part in range(x.shape[0]):
            o[e, part * height : (part + 1) * height, :] = x[part, e]


def stack_columns(x, *refs):
    o = refs[-1]
    height = o.shape[1]
    pieces = x.shape[2] // height

    @pl.loop(0, x.shape[1])
    def _(e):
        for part in range(x.shape[0]):
            for piece in range(pieces):
                start = (part * pieces + piece) * LANES
                o[e, :, start : start + LANES] = x[part, e, piece * height : (piece + 1) * height, :]


def per_expert(shape, first=0):
    return pl.BlockSpec((STEP,) + shape[1:], lambda e: (e + first // STEP, 0, 0))


def per_expert_parts(shape, first=0):
    return pl.BlockSpec((shape[0], STEP) + shape[2:], lambda e: (0, e + first // STEP, 0, 0))


def call(body, count, inputs, specs, out, out_spec, held):
    aliases = {}
    if held is not None:
        aliases = {len(inputs): 0}
        inputs, specs = (*inputs, held), (*specs, pl.BlockSpec(memory_space=pl.ANY))
    moved = int(count * 2**21)
    return pl.pallas_call(
        body,
        grid=(count // STEP,),
        in_specs=list(specs),
        out_specs=out_spec,
        out_shape=out,
        input_output_aliases=aliases,
        cost_estimate=pl.CostEstimate(flops=moved, bytes_accessed=moved, transcendentals=0),
        compiler_params=pltpu.CompilerParams(
            dimension_semantics=("arbitrary",), vmem_limit_bytes=50 * 2**20
        ),
    )(*inputs)


def partial_sums(body, w, a, length, first, count):
    out = jax.ShapeDtypeStruct((count, 1, length), jnp.float32)
    specs = (per_expert(w.shape, first), per_expert(a.shape, first))
    return call(body, count, (w, a), specs, out, per_expert(out.shape), None)


def normalised(body, w, a, first, scale, scale_first, count, shape, slot=0, held=None):
    out = jax.ShapeDtypeStruct(shape, jnp.bfloat16)
    specs = (per_expert(w.shape, first), per_expert(a.shape, first), per_expert(scale.shape, scale_first))
    return call(body, count, (w, a, scale), specs, out, per_expert_parts(shape, slot), held)


def placed(body, x, slot, count, shape, first=0, held=None):
    out = jax.ShapeDtypeStruct(shape, jnp.bfloat16)
    return call(body, count, (x,), (per_expert_parts(x.shape, slot),), out, per_expert(shape, first), held)


def exchanged(x):
    return lax.all_to_all(x, "rows", split_axis=0, concat_axis=0, tiled=True)


def shards(parts, w_gate, avg_gate, w_up, avg_up, w_down, avg_down, router_weight, router_gain):
    experts, high, wide = w_gate.shape
    tall, deep = w_down.shape[1:]
    block, slab = wide // parts, tall // parts
    rank = lax.axis_index("rows")
    early = experts * 3 // 4 // STEP * STEP
    late = experts // 2 // STEP * STEP
    kept = experts - early

    part_router = (router_weight * router_gain[:, None]).astype(jnp.bfloat16).astype(jnp.float32).T
    columns, rows = part_router.shape
    head = partial_sums(columns_sum, w_gate, avg_gate, wide, 0, early)
    gathered = lax.all_gather(
        jnp.concatenate((head, part_router.reshape(-1, 1, wide))), "rows"
    )
    scale_head = jnp.sqrt(jnp.sum(gathered[:, :early], axis=0))
    row_router = gathered[:, early:].reshape(parts, columns, rows)

    send_a = normalised(
        columns_norm, w_gate, avg_gate, 0, scale_head, 0, early, (parts, early, high, block)
    )
    send_a, w_up, avg_up, w_down, avg_down, w_gate, avg_gate = lax.optimization_barrier(
        (send_a, w_up, avg_up, w_down, avg_down, w_gate, avg_gate)
    )
    got_a = exchanged(send_a)

    part_rest = partial_sums(columns_sum, w_gate, avg_gate, wide, early, kept)
    part_up = partial_sums(columns_sum, w_up, avg_up, wide, 0, experts)
    part_down = partial_sums(rows_sum, w_down, avg_down, tall, 0, experts)
    total_columns, total_down = lax.psum(
        (jnp.concatenate((part_up, part_rest)), part_down), "rows"
    )
    scale_columns, scale_down = jnp.sqrt(total_columns), jnp.sqrt(total_down)
    scale_up, scale_rest = scale_columns[:experts], scale_columns[experts:]
    shape_b = (parts, kept + experts + late, high, block)
    send_b = normalised(columns_norm, w_gate, avg_gate, early, scale_columns, experts, kept, shape_b)
    send_b = normalised(columns_norm, w_up, avg_up, 0, scale_columns, 0, experts, shape_b, kept, send_b)
    send_b = normalised(
        rows_norm, w_down, avg_down, 0, scale_down, 0, late, shape_b, kept + experts, send_b
    )
    send_b, scale_last = lax.optimization_barrier((send_b, scale_down))
    got_b = exchanged(send_b)

    last = experts - late
    send_c = normalised(
        rows_norm, w_down, avg_down, late, scale_last, late, last, (parts, last, high, block)
    )
    shape_columns = (experts, high * parts, block)
    shape_down = (experts, slab, deep * parts)
    serve_gate = placed(stack_rows, got_a, 0, early, shape_columns)
    row_router, send_c = lax.optimization_barrier((row_router, send_c))
    got_c = exchanged(send_c)
    row_router = row_router.transpose(1, 0, 2).reshape(columns, parts * rows).astype(jnp.bfloat16)
    serve_router = lax.all_gather(row_router, "owner", axis=0, tiled=True).T

    serve_gate = placed(stack_rows, got_b, 0, kept, shape_columns, early, serve_gate)
    serve_up = placed(stack_rows, got_b, kept, experts, shape_columns)
    serve_down = placed(stack_columns, got_b, kept + experts, late, shape_down)
    serve_down = placed(stack_columns, got_c, 0, last, shape_down, late, serve_down)

    def own(scale, width):
        return lax.dynamic_slice_in_dim(scale[:, 0, :], rank * width, width, axis=1)

    return (
        serve_gate,
        serve_up,
        serve_down,
        own(jnp.concatenate((scale_head, scale_rest)), block),
        own(scale_up, block),
        own(scale_down, slab),
        serve_router,
    )


def plain_shards(w_gate, avg_gate, w_up, avg_up, w_down, avg_down, router_weight, router_gain):
    def served(w, a, axis, split):
        fresh = w + a.astype(jnp.float32)
        scale = jnp.sqrt(lax.psum(jnp.sum(fresh * fresh, axis=axis), "rows"))
        narrow = (fresh / jnp.expand_dims(scale, axis)).astype(jnp.bfloat16)
        serve = lax.all_to_all(narrow, "rows", split_axis=split, concat_axis=axis, tiled=True)
        width = serve.shape[split]
        return serve, lax.dynamic_slice_in_dim(scale, lax.axis_index("rows") * width, width, axis=1)

    serve_gate, scale_gate = served(w_gate, avg_gate, 1, 2)
    serve_up, scale_up = served(w_up, avg_up, 1, 2)
    serve_down, scale_down = served(w_down, avg_down, 2, 1)
    part_router = (router_weight * router_gain[:, None]).astype(jnp.bfloat16)
    row_router = lax.all_gather(part_router, "rows", axis=0, tiled=True)
    serve_router = lax.all_gather(row_router, "owner", axis=1, tiled=True)
    return (serve_gate, serve_up, serve_down, scale_gate, scale_up, scale_down, serve_router)


def solution(mesh):
    parts = mesh.shape["rows"]

    def dispatched(*args):
        experts, high, wide = args[0].shape
        tall, deep = args[4].shape[1:]
        block, slab = wide // parts, tall // parts
        aligned = block == LANES and slab % LANES == 0 and deep % LANES == 0
        aligned = aligned and slab * deep == high * block and experts % STEP == 0
        aligned = aligned and experts >= 2 * STEP and args[6].size % wide == 0
        return shards(parts, *args) if aligned else plain_shards(*args)

    return jax.shard_map(
        dispatched,
        mesh=mesh,
        in_specs=(
            P("owner", "rows", None),
            P("owner", "rows", None),
            P("owner", "rows", None),
            P("owner", "rows", None),
            P("owner", None, "rows"),
            P("owner", None, "rows"),
            P("rows", "owner"),
            P("rows"),
        ),
        out_specs=(
            P("owner", None, "rows"),
            P("owner", None, "rows"),
            P("owner", "rows", None),
            P("owner", "rows"),
            P("owner", "rows"),
            P("owner", "rows"),
            P(),
        ),
        check_vma=False,
    )
```

profile of v0, /device:TPU:0, one launch (start us, length us, event | category | flops | bytes accessed | tf_op | source)
XLA Modules:
  0.0 624.2 jit_solution(1997259938808066041)
XLA Ops:
  7.2 0.7 convert_bitcast_fusion
  7.9 7.9 %shard_map.135 = f32[12,1,1024]{2,1,0:T(1,128)S(1)} custom-call(f32[16,256,1024]{2,1,0:T(8,128)} %w.7, bf16[16,256,1024]{2,1,0:T(8,128)(2,1)} %a.7), custom_call_target="tpu_custom_call" | custom-call | flops 25165824 | bytes 25165824 | tf_op jit(solution)/shard_map/pallas_call | solution.py:93
  15.8 0.1 pad_maximum_fusion.1
  15.9 16.5 %all-gather = f32[128,1,1024]{2,1,0:T(1,128)S(1)} all-gather(f32[16,1,1024]{2,1,0:T(1,128)S(1)} %pad_maximum_fusion.1), channel_id=2, replica_groups=mesh['owner'=4,'rows'=8] {'rows'}, dimensions={0}, use_global_device_ids=true | all-gather | bytes 589824 | tf_op jit(solution)/shard_map/all_gather | solution.py:140
  32.4 0.2 slice_reduce_fusion
  32.7 10.0 %shard_map.136 = bf16[8,12,256,128]{3,2,1,0:T(8,128)(2,1)} custom-call(f32[16,256,1024]{2,1,0:T(8,128)} %w.7, bf16[16,256,1024]{2,1,0:T(8,128)(2,1)} %a.7, f32[12,1,1024]{2,1,0:T(1,128)S(1)} %sqrt.12.s), custom_call_target="tpu_custom_call" | custom-call | flops 25165824 | bytes 25165824 | tf_op jit(solution)/shard_map/pallas_call | solution.py:93
  42.7 4.8 all-to-all-start.1
  47.5 0.0 all-reduce.3.cloned.1.call-start
  47.6 3.9 shard_map.139
  51.4 9.8 %shard_map.138 = f32[16,1,1024]{2,1,0:T(1,128)S(1)} custom-call(f32[16,256,1024]{2,1,0:T(8,128)} %w.8, bf16[16,256,1024]{2,1,0:T(8,128)(2,1)} %a.8), custom_call_target="tpu_custom_call" | custom-call | flops 33554432 | bytes 33554432 | tf_op jit(solution)/shard_map/pallas_call | solution.py:93
  61.2 10.1 %shard_map.137 = f32[16,1,1024]{2,1,0:T(1,128)} custom-call(f32[16,1024,256]{2,1,0:T(8,128)} %w.10, bf16[16,1024,256]{2,1,0:T(8,128)(2,1)} %a.10), custom_call_target="tpu_custom_call" | custom-call | flops 33554432 | bytes 33554432 | tf_op jit(solution)/shard_map/pallas_call | solution.py:93
  71.3 0.7 pad_maximum_fusion
  72.0 0.0 all-reduce.3.cloned.1.call-update
  72.0 61.4 %all-reduce.3.cloned.1.call-done = (f32[16,1,1024]{2,1,0:T(1,128)}, f32[20,1,1024]{2,1,0:T(1,128)}) async-done(((f32[16,1,1024]{2,1,0:T(1,128)}, f32[20,1,1024]{2,1,0:T(1,128)}), (f32[16,1,1024]{2,1,0:T(1,128)}, f32[20,1,1024]{2,1,0:T(1,128)})) %all-reduce.3.cloned.1.call-update) | async-done | bytes 147472 | tf_op jit(solution)/shard_map/psum | solution.py:157
  133.5 1.0 sqrt.14.s
  134.5 1.0 sqrt.13.s
  135.5 4.8 shard_map.140.refs_0_
  140.3 12.1 %shard_map.141.refs_0_ = bf16[8,28,256,128]{3,2,1,0:T(8,128)(2,1)} custom-call(f32[16,256,1024]{2,1,0:T(8,128)} %w.8, bf16[16,256,1024]{2,1,0:T(8,128)(2,1)} %a.8, f32[20,1,1024]{2,1,0:T(1,128)S(1)} %sqrt.14.s, bf16[8,28,256,128]{3,2,1,0:T(8,128)(2,1)} %shard_map.140.refs_0_), custom_call_target="tpu_custom_call", output_to_operand_aliasing={{}: (3, {})} | custom-call | flops 33554432 | bytes 33554432 | tf_op jit(solution)/shard_map/pallas_call | solution.py:93
  152.4 6.9 %shard_map.142 = bf16[8,28,256,128]{3,2,1,0:T(8,128)(2,1)} custom-call(f32[16,1024,256]{2,1,0:T(8,128)} %w.10, bf16[16,1024,256]{2,1,0:T(8,128)(2,1)} %a.10, f32[16,1,1024]{2,1,0:T(1,128)S(1)} %sqrt.13.s, bf16[8,28,256,128]{3,2,1,0:T(8,128)(2,1)} %shard_map.141.refs_0_), custom_call_target="tpu_custom_call", output_to_operand_aliasing={{}: (3, {})} | custom-call | flops 16777216 | bytes 16777216 | tf_op jit(solution)/shard_map/pallas_call | solution.py:93
  159.2 30.5 %all-to-all-done.1.x = bf16[8,12,256,128]{3,2,1,0:T(8,128)(2,1)} async-done(((bf16[8,12,256,128]{3,2,1,0:T(8,128)(2,1)}), bf16[8,12,256,128]{3,2,1,0:T(8,128)(2,1)}, u32[]{:S(2)}, u32[]{:S(2)}) %all-to-all-start.1) | async-done | bytes 6291488 | tf_op jit(solution)/shard_map/all_to_all | solution.py:125
  189.7 5.6 all-to-all-start
  195.3 0.4 slice_reduce_fusion.1
  195.7 6.9 %shard_map.146 = bf16[8,8,256,128]{3,2,1,0:T(8,128)(2,1)} custom-call(f32[16,1024,256]{2,1,0:T(8,128)} %w.10, bf16[16,1024,256]{2,1,0:T(8,128)(2,1)} %a.10, f32[16,1,1024]{2,1,0:T(1,128)S(1)} %sqrt.13.s), custom_call_target="tpu_custom_call" | custom-call | flops 16777216 | bytes 16777216 | tf_op jit(solution)/shard_map/pallas_call | solution.py:93
  202.6 311.4 %all-to-all-done.x = bf16[8,28,256,128]{3,2,1,0:T(8,128)(2,1)} async-done(((bf16[8,28,256,128]{3,2,1,0:T(8,128)(2,1)}), bf16[8,28,256,128]{3,2,1,0:T(8,128)(2,1)}, u32[]{:S(2)}, u32[]{:S(2)}) %all-to-all-start) | async-done | bytes 14680096 | tf_op jit(solution)/shard_map/all_to_all | solution.py:125
  514.0 4.6 all-to-all-start.2
  518.7 9.0 %all_gather.11 = bf16[64,2048]{1,0:T(8,128)(2,1)S(1)} all-gather(bf16[16,2048]{1,0:T(8,128)(2,1)S(1)} %bitcast.13), channel_id=1, replica_groups=mesh['owner'=4,'rows'=8] {'owner'}, dimensions={0}, use_global_device_ids=true | all-gather | bytes 327680 | tf_op jit(solution)/shard_map/all_gather | solution.py:181
  527.6 0.6 constant_dynamic-slice_fusion.1
  528.3 0.6 fusion
  528.9 6.4 %shard_map.143.refs_0_ = bf16[16,2048,128]{2,1,0:T(8,128)(2,1)} custom-call(bf16[8,12,256,128]{3,2,1,0:T(8,128)(2,1)} %all-to-all-done.1.x), custom_call_target="tpu_custom_call" | custom-call | flops 25165824 | bytes 25165824 | tf_op jit(solution)/shard_map/pallas_call | solution.py:93
  535.3 3.0 shard_map.144
  538.3 4.1 shard_map.147.refs_0_
  542.5 7.1 %shard_map.145 = bf16[16,2048,128]{2,1,0:T(8,128)(2,1)} custom-call(bf16[8,28,256,128]{3,2,1,0:T(8,128)(2,1)} %all-to-all-done.x), custom_call_target="tpu_custom_call" | custom-call | flops 33554432 | bytes 33554432 | tf_op jit(solution)/shard_map/pallas_call | solution.py:93
  549.6 62.9 %all-to-all-done.2.x = bf16[8,8,256,128]{3,2,1,0:T(8,128)(2,1)} async-done(((bf16[8,8,256,128]{3,2,1,0:T(8,128)(2,1)}), bf16[8,8,256,128]{3,2,1,0:T(8,128)(2,1)}, u32[]{:S(2)}, u32[]{:S(2)}) %all-to-all-start.2) | async-done | bytes 4194336 | tf_op jit(solution)/shard_map/all_to_all | solution.py:125
  612.6 4.1 shard_map.148
  616.7 0.7 copy.31
  (8 shorter events, 0.2 us)
Async XLA Ops:
  42.7 147.0 %all-to-all-start.1 = ((bf16[8,12,256,128]{3,2,1,0:T(8,128)(2,1)}), bf16[8,12,256,128]{3,2,1,0:T(8,128)(2,1)}, u32[]{:S(2)}, u32[]{:S(2)}) async-start(bf16[8,12,256,128]{3,2,1,0:T(8,128)(2,1)} %shard_map.136), calls=%async_computation.1 | async-start | bytes 12582912 | tf_op jit(solution)/shard_map/all_to_all | solution.py:125
  47.5 86.0 %all-reduce.3.cloned.1.call-start = ((), (), s32[]{:S(2)}) async-start(), calls=%async_computation.3 | async-start | bytes 294912 | tf_op jit(solution)/shard_map/psum | solution.py:157
  189.7 324.2 %all-to-all-start = ((bf16[8,28,256,128]{3,2,1,0:T(8,128)(2,1)}), bf16[8,28,256,128]{3,2,1,0:T(8,128)(2,1)}, u32[]{:S(2)}, u32[]{:S(2)}) async-start(bf16[8,28,256,128]{3,2,1,0:T(8,128)(2,1)} %shard_map.142), calls=%async_computation | async-start | bytes 29360128 | tf_op jit(solution)/shard_map/all_to_all | solution.py:125
  514.0 98.6 %all-to-all-start.2 = ((bf16[8,8,256,128]{3,2,1,0:T(8,128)(2,1)}), bf16[8,8,256,128]{3,2,1,0:T(8,128)(2,1)}, u32[]{:S(2)}, u32[]{:S(2)}) async-start(bf16[8,8,256,128]{3,2,1,0:T(8,128)(2,1)} %shard_map.146), calls=%async_computation.2 | async-start | bytes 8388608 | tf_op jit(solution)/shard_map/all_to_all | solution.py:125
Sparse Core Ops, SparseCore 0:
  72.2 61.2 all-reduce.2
where the time goes:
time: 625 us; the launch traced here: 624 us
  waiting for transfers between devices  466 us (75%)
  Pallas kernels  97.2 us (16%)
  blocking collectives  25.5 us (4%)
  starting transfers between devices  15 us (2%)
  between operations  14.2 us (2%)
    all_to_all x3, waiting for transfers between devices, exchanged(): return lax.all_to_all(x, 'rows', split_axis=0, concat_axis=0, tiled=True)  405 us
    pallas_call x14, Pallas kernels, call(): pl.pallas_call(body, grid=(count // STEP,), in_specs=list(specs), out_spe...  97.2 us
    psum x1, waiting for transfers between devices, shards(): lax.psum((jnp.concatenate((part_up, part_rest)), part_down), 'rows')  61.4 us
    all_gather x1, blocking collectives, shards(): lax.all_gather(jnp.concatenate((head, part_router.reshape(-1, 1, wide))),...  16.5 us
    all_to_all x3, starting transfers between devices, exchanged(): return lax.all_to_all(x, 'rows', split_axis=0, concat_axis=0, tiled=True)  14.9 us
  transfers between devices with their start and end apart: 4, of which 4 were waited for; matrix products, arithmetic and copies ran while one was open for 1% of the time, Pallas kernels for 12%

commit v1 on v0

v1 whole, which is shorter than its diff:
```python
import functools

import jax
import jax.numpy as jnp
from jax import lax
from jax.experimental import pallas as pl
from jax.experimental.pallas import tpu as pltpu
from jax.sharding import PartitionSpec as P

LANES = 128
HEAD = 3
NEXT = 3
RING = 4
TAIL = 2
MESH = pl.DeviceIdType.MESH


def remote(src, dst, send, recv, peer, axis="rows"):
    return pltpu.make_async_remote_copy(
        src_ref=src, dst_ref=dst, send_sem=send, recv_sem=recv, device_id={axis: peer}, device_id_type=MESH
    )


def regroup(
    parts, owners,
    wg, ag, wu, au, wd, ad, rw, gain,
    og, ou, od, ot, oscale, orouter,
    wbuf, abuf, wdbuf, adbuf, sg, su, sd, part, heard, factors, scales, rwbuf, gainbuf, piece, router,
    in_sem, down_sem, sum_send, sum_recv, factor_send, factor_recv, data_send, data_recv, kept, piece_send, piece_recv,
    router_send, router_recv, small,
):
    me = lax.axis_index("rows")
    own = lax.axis_index("owner")
    experts, high = wg.shape[0], wg.shape[1]
    tall, deep = wd.shape[1:]
    units = 3 * experts
    tail = ot.shape[1]

    def peer(k):
        return lax.rem(me + k, parts)

    def fetch(w, a, e, wv, av, sem, slot):
        pltpu.make_async_copy(w.at[e], wv.at[slot], sem.at[0, slot]).start()
        pltpu.make_async_copy(a.at[e], av.at[slot], sem.at[1, slot]).start()

    def fetched(w, a, e, wv, av, sem, slot):
        pltpu.make_async_copy(w.at[e], wv.at[slot], sem.at[0, slot]).wait()
        pltpu.make_async_copy(a.at[e], av.at[slot], sem.at[1, slot]).wait()

    def stream(w, a, wv, av, sem, base, first, count, body):
        for i in range(min(RING - 1, count)):
            fetch(w, a, first + i, wv, av, sem, base + i)

        @pl.loop(0, count)
        def _(i):
            slot = base + lax.rem(i, RING)
            fetched(w, a, first + i, wv, av, sem, slot)

            @pl.when(i + RING - 1 < count)
            def _():
                fetch(w, a, first + i + RING - 1, wv, av, sem, base + lax.rem(i + RING - 1, RING))

            body(first + i, slot)

    def lanes(p):
        return pl.ds(pl.multiple_of(p * LANES, LANES), LANES)

    def columns_sum(unit, slot):
        @pl.loop(0, parts)
        def _(p):
            fresh = wbuf[slot, :, lanes(p)] + abuf[slot, :, lanes(p)].astype(jnp.float32)
            part[p, unit] = jnp.sum(fresh * fresh, axis=0, keepdims=True)

    def rows_sum(unit, slot):
        @pl.loop(0, parts)
        def _(p):
            fresh = wdbuf[slot, lanes(p), :] + adbuf[slot, lanes(p), :].astype(jnp.float32)
            square = fresh * fresh
            folded = square[:, :LANES]
            for start in range(LANES, deep, LANES):
                folded = folded + square[:, start : start + LANES]
            part[p, unit] = jnp.sum(folded.T, axis=0, keepdims=True)

    def columns_norm(unit, e, slot, send):
        @pl.loop(0, parts)
        def _(p):
            fresh = wbuf[slot, :, lanes(p)] + abuf[slot, :, lanes(p)].astype(jnp.float32)
            send[e, p] = (fresh * factors[p, unit]).astype(send.dtype)

    def rows_norm(unit, e, slot):
        @pl.loop(0, parts)
        def _(p):
            factor = jnp.broadcast_to(factors[p, unit], (LANES, LANES)).T
            for start in range(0, deep, LANES):
                fresh = wdbuf[slot, lanes(p), start : start + LANES]
                fresh = fresh + adbuf[slot, lanes(p), start : start + LANES].astype(jnp.float32)
                sd[e, p, :, start : start + LANES] = (fresh * factor).astype(sd.dtype)

    def send_sums(group, first, count):
        @pl.loop(1, parts)
        def _(k):
            remote(
                part.at[peer(k), pl.ds(first, count)], heard.at[me, pl.ds(first, count)],
                sum_send.at[group], sum_recv.at[group], peer(k),
            ).start()

    def send_factors(group, first, count):
        whole = heard.at[pl.ds(0, parts - 1), pl.ds(first, count)]
        pltpu.make_async_copy(whole, whole, sum_recv.at[group]).wait()

        @pl.loop(first, first + count)
        def _(unit):
            total = part[me, unit]
            for k in range(1, parts):
                total = total + heard[peer(k), unit]
            scale = jnp.sqrt(total)
            scales[unit] = scale
            factors[me, unit] = 1.0 / scale

        @pl.loop(1, parts)
        def _(k):
            mine = factors.at[me, pl.ds(first, count)]
            remote(mine, mine, factor_send.at[group], factor_recv.at[group], peer(k)).start()

    def take_factors(group, first, count):
        whole = factors.at[pl.ds(0, parts - 1), pl.ds(first, count)]
        pltpu.make_async_copy(whole, whole, factor_recv.at[group]).wait()

    def push(kind, e):
        send, stage = ((sg, og), (su, ou), (sd, od))[kind]
        if kind < 2:
            place = stage.at[e, pl.ds(pl.multiple_of(me * high, high), high), :]
        else:
            place = stage.at[e, :, pl.ds(pl.multiple_of(me * deep, deep), deep)]

        @pl.loop(1, parts)
        def _(k):
            remote(send.at[e, peer(k)], place, data_send.at[kind], data_recv.at[kind], peer(k)).start()

        pltpu.make_async_copy(send.at[e, me], place, kept.at[kind]).start()

    barrier = pltpu.get_barrier_semaphore()
    early = HEAD + NEXT
    for i in range(early):
        fetch(wg, ag, i, wbuf, abuf, in_sem, i)
    pltpu.make_async_copy(rw, rwbuf, small.at[0]).start()
    pltpu.make_async_copy(gain, gainbuf, small.at[1]).start()

    @pl.loop(1, parts)
    def _(k):
        pl.semaphore_signal(barrier, inc=1, device_id={"rows": peer(k)}, device_id_type=MESH)

    for k in range(1, owners):
        pl.semaphore_signal(barrier, inc=1, device_id={"owner": lax.rem(own + k, owners)}, device_id_type=MESH)

    @pl.loop(0, HEAD)
    def _(i):
        fetched(wg, ag, i, wbuf, abuf, in_sem, i)
        columns_sum(i, i)

    pl.semaphore_wait(barrier, parts - 1 + owners - 1)
    send_sums(0, 0, HEAD)

    pltpu.make_async_copy(rw, rwbuf, small.at[0]).wait()
    pltpu.make_async_copy(gain, gainbuf, small.at[1]).wait()
    piece[...] = (rwbuf[...] * gainbuf[...]).astype(piece.dtype)

    @pl.loop(HEAD, early)
    def _(i):
        fetched(wg, ag, i, wbuf, abuf, in_sem, i)
        columns_sum(i, i)

    strip = router.at[own, :, pl.ds(pl.multiple_of(me * high, high), high)]
    send_factors(0, 0, HEAD)
    send_sums(1, HEAD, NEXT)
    take_factors(0, 0, HEAD)

    columns_norm(0, 0, 0, sg)
    columns_norm(1, 1, 1, sg)
    push(0, 0)
    send_factors(1, HEAD, NEXT)
    columns_norm(2, 2, 2, sg)
    push(0, 1)

    @pl.loop(1, parts)
    def _(k):
        remote(piece, strip, piece_send, piece_recv, peer(k)).start()

    router[own, :, pl.ds(pl.multiple_of(me * high, high), high)] = piece[...]
    push(0, 2)

    stream(wg, ag, wbuf, abuf, in_sem, early, early, experts - early, columns_sum)
    stream(wu, au, wbuf, abuf, in_sem, early, 0, experts, lambda e, slot: columns_sum(experts + e, slot))
    stream(wd, ad, wdbuf, adbuf, down_sem, 0, 0, experts, lambda e, slot: rows_sum(2 * experts + e, slot))

    send_sums(2, early, units - early)
    take_factors(1, HEAD, NEXT)

    @pl.loop(HEAD, early)
    def _(i):
        columns_norm(i, i, i, sg)

    push(0, HEAD)
    send_factors(2, early, units - early)

    @pl.loop(HEAD + 1, early)
    def _(i):
        push(0, i)

    gathered = router.at[own, :, pl.ds(0, (parts - 1) * high)]
    pltpu.make_async_copy(gathered, gathered, piece_recv).wait()
    for k in range(1, owners):
        remote(
            router.at[own], router.at[own], router_send, router_recv, lax.rem(own + k, owners), "owner"
        ).start()

    pltpu.make_async_copy(scales, oscale, small.at[0]).start()
    take_factors(2, early, units - early)

    def gate(e, slot):
        columns_norm(e, e, slot, sg)

        @pl.when(e > early)
        def _():
            push(0, e - 1)

    def up(e, slot):
        columns_norm(experts + e, e, slot, su)

        @pl.when(e > 0)
        def _():
            push(1, e - 1)

    def down(e, slot):
        rows_norm(2 * experts + e, e, slot)

        @pl.when((e > 0) & (e <= experts - tail))
        def _():
            push(2, e - 1)

    stream(wg, ag, wbuf, abuf, in_sem, early, early, experts - early, gate)
    push(0, experts - 1)
    stream(wu, au, wbuf, abuf, in_sem, early, 0, experts, up)
    push(1, experts - 1)
    stream(wd, ad, wdbuf, adbuf, down_sem, 0, 0, experts, down)

    for i in range(tail):
        pltpu.make_async_copy(sd.at[experts - tail + i], ot.at[:, i], kept.at[3]).start()

    arrived = router.at[pl.ds(0, owners - 1)]
    pltpu.make_async_copy(arrived, arrived, router_recv).wait()
    pltpu.make_async_copy(router, orouter, small.at[1]).start()

    for group, first, count in ((0, 0, HEAD), (1, HEAD, NEXT), (2, early, units - early)):
        whole = part.at[pl.ds(0, parts - 1), pl.ds(first, count)]
        pltpu.make_async_copy(whole, whole, sum_send.at[group]).wait()
        pltpu.make_async_copy(whole, whole, factor_send.at[group]).wait()
    pltpu.make_async_copy(gathered, gathered, piece_send).wait()
    pltpu.make_async_copy(arrived, arrived, router_send).wait()
    pltpu.make_async_copy(scales, oscale, small.at[0]).wait()
    pltpu.make_async_copy(router, orouter, small.at[1]).wait()
    pltpu.make_async_copy(sd.at[pl.ds(experts - tail, tail)], sd.at[pl.ds(experts - tail, tail)], kept.at[3]).wait()
    for kind, (send, stage) in enumerate(((sg, og), (su, ou), (sd, od))):
        count = experts - tail if kind == 2 else experts
        pltpu.make_async_copy(send.at[pl.ds(0, count), 0], send.at[pl.ds(0, count), 0], kept.at[kind]).wait()
        most = send.at[pl.ds(0, count), pl.ds(0, parts - 1)]
        pltpu.make_async_copy(most, most, data_send.at[kind]).wait()
        pltpu.make_async_copy(most, most, data_recv.at[kind]).wait()


def copied(x, *refs):
    refs[-1][...] = x[...]


def stack_columns(x, *refs):
    o = refs[-1]
    deep = x.shape[3]
    for source in range(x.shape[0]):
        o[:, :, source * deep : (source + 1) * deep] = x[source]


def placed(body, count, step, x, x_spec, out_shape, first=0, held=None):
    inputs, specs, aliases = [x], [x_spec], {}
    if held is not None:
        inputs, specs, aliases = [x, held], [x_spec, pl.BlockSpec(memory_space=pl.ANY)], {1: 0}
    moved = int(count * 2**21)
    return pl.pallas_call(
        body,
        grid=(count // step,),
        in_specs=specs,
        out_specs=pl.BlockSpec((step,) + out_shape[1:], lambda e: (e + first // step, 0, 0)),
        out_shape=jax.ShapeDtypeStruct(out_shape, jnp.bfloat16),
        input_output_aliases=aliases,
        cost_estimate=pl.CostEstimate(flops=moved, bytes_accessed=moved, transcendentals=0),
        compiler_params=pltpu.CompilerParams(
            dimension_semantics=("arbitrary",), vmem_limit_bytes=50 * 2**20
        ),
    )(*inputs)


def whole_experts(shape, step):
    return pl.BlockSpec((step,) + shape[1:], lambda e: (e, 0, 0))


def shards(parts, owners, w_gate, avg_gate, w_up, avg_up, w_down, avg_down, router_weight, router_gain):
    experts, high, wide = w_gate.shape
    tall, deep = w_down.shape[1:]
    block, slab = wide // parts, tall // parts
    units, slots = 3 * experts, HEAD + NEXT + RING
    columns = router_weight.shape[1]
    f32, bf16 = jnp.float32, jnp.bfloat16
    any_spec = pl.BlockSpec(memory_space=pl.ANY)
    shape_columns, shape_down = (experts, high * parts, block), (experts, slab, deep * parts)
    dma = pltpu.SemaphoreType.DMA

    stage_gate, stage_up, stage_down, last, scales, routers = pl.pallas_call(
        functools.partial(regroup, parts, owners),
        in_specs=[any_spec] * 8,
        out_specs=[any_spec] * 6,
        out_shape=[
            jax.ShapeDtypeStruct(shape_columns, bf16),
            jax.ShapeDtypeStruct(shape_columns, bf16),
            jax.ShapeDtypeStruct(shape_down, bf16),
            jax.ShapeDtypeStruct((parts, TAIL, slab, deep), bf16),
            jax.ShapeDtypeStruct((units, 1, LANES), f32),
            jax.ShapeDtypeStruct((owners, columns, parts * high), bf16),
        ],
        scratch_shapes=[
            pltpu.VMEM((slots, high, wide), f32),
            pltpu.VMEM((slots, high, wide), bf16),
            pltpu.VMEM((RING, tall, deep), f32),
            pltpu.VMEM((RING, tall, deep), bf16),
            pltpu.VMEM((experts, parts, high, block), bf16),
            pltpu.VMEM((experts, parts, high, block), bf16),
            pltpu.VMEM((experts, parts, slab, deep), bf16),
            pltpu.VMEM((parts, units, 1, LANES), f32),
            pltpu.VMEM((parts, units, 1, LANES), f32),
            pltpu.VMEM((parts, units, 1, LANES), f32),
            pltpu.VMEM((units, 1, LANES), f32),
            pltpu.VMEM((columns, high), f32),
            pltpu.VMEM((1, high), f32),
            pltpu.VMEM((columns, high), bf16),
            pltpu.VMEM((owners, columns, parts * high), bf16),
            dma((2, slots)), dma((2, RING)),
            dma((3,)), dma((3,)), dma((3,)), dma((3,)),
            dma((3,)), dma((3,)), dma((4,)),
            dma, dma, dma, dma, dma((2,)),
        ],
        cost_estimate=pl.CostEstimate(flops=2**30, bytes_accessed=2**28, transcendentals=0),
        compiler_params=pltpu.CompilerParams(
            collective_id=0, has_side_effects=True, vmem_limit_bytes=60 * 2**20
        ),
    )(w_gate, avg_gate, w_up, avg_up, w_down, avg_down, router_weight.T, router_gain.reshape(1, high))

    got = lax.all_to_all(last, "rows", split_axis=0, concat_axis=0, tiled=True)
    step = 2
    serve_gate = placed(copied, experts, step, stage_gate, whole_experts(shape_columns, step), shape_columns)
    serve_up = placed(copied, experts, step, stage_up, whole_experts(shape_columns, step), shape_columns)
    serve_down = placed(copied, experts - TAIL, step, stage_down, whole_experts(shape_down, step), shape_down)
    serve_router = routers.reshape(owners * columns, parts * high).T
    scales = scales.reshape(3, experts, LANES)
    serve_down = placed(
        stack_columns, TAIL, TAIL, got, pl.BlockSpec(got.shape, lambda e: (0, 0, 0, 0)), shape_down,
        experts - TAIL, serve_down,
    )
    return (serve_gate, serve_up, serve_down, scales[0], scales[1], scales[2], serve_router)


def plain_shards(w_gate, avg_gate, w_up, avg_up, w_down, avg_down, router_weight, router_gain):
    def served(w, a, axis, split):
        fresh = w + a.astype(jnp.float32)
        scale = jnp.sqrt(lax.psum(jnp.sum(fresh * fresh, axis=axis), "rows"))
        narrow = (fresh / jnp.expand_dims(scale, axis)).astype(jnp.bfloat16)
        serve = lax.all_to_all(narrow, "rows", split_axis=split, concat_axis=axis, tiled=True)
        width = serve.shape[split]
        return serve, lax.dynamic_slice_in_dim(scale, lax.axis_index("rows") * width, width, axis=1)

    serve_gate, scale_gate = served(w_gate, avg_gate, 1, 2)
    serve_up, scale_up = served(w_up, avg_up, 1, 2)
    serve_down, scale_down = served(w_down, avg_down, 2, 1)
    part_router = (router_weight * router_gain[:, None]).astype(jnp.bfloat16)
    row_router = lax.all_gather(part_router, "rows", axis=0, tiled=True)
    serve_router = lax.all_gather(row_router, "owner", axis=1, tiled=True)
    return (serve_gate, serve_up, serve_down, scale_gate, scale_up, scale_down, serve_router)


def solution(mesh):
    parts, owners = mesh.shape["rows"], mesh.shape["owner"]

    def dispatched(*args):
        experts, high, wide = args[0].shape
        tall, deep = args[4].shape[1:]
        block, slab = wide // parts, tall // parts
        columns = args[6].shape[1]
        aligned = block == LANES and slab == LANES and deep % LANES == 0 and high % LANES == 0
        aligned = aligned and high <= 256 and deep <= 256 and experts <= 16 and experts % 2 == 0
        aligned = aligned and experts > HEAD + NEXT and columns % 16 == 0 and parts > 1 and owners > 1
        return shards(parts, owners, *args) if aligned else plain_shards(*args)

    return jax.shard_map(
        dispatched,
        mesh=mesh,
        in_specs=(
            P("owner", "rows", None),
            P("owner", "rows", None),
            P("owner", "rows", None),
            P("owner", "rows", None),
            P("owner", None, "rows"),
            P("owner", None, "rows"),
            P("rows", "owner"),
            P("rows"),
        ),
        out_specs=(
            P("owner", None, "rows"),
            P("owner", None, "rows"),
            P("owner", "rows", None),
            P("owner", "rows"),
            P("owner", "rows"),
            P("owner", "rows"),
            P(),
        ),
        check_vma=False,
    )
```

time: 625 us -> 576 us (0.922)
  Pallas kernels: 97.2 us -> 567 us
  waiting for transfers between devices: 466 us -> 0.01 us
  blocking collectives: 25.5 us -> 0 us
  between operations: 14.2 us -> 0.65 us
  starting transfers between devices: 15 us -> 6.36 us
    pallas_call x14 -> x5, Pallas kernels: 97.2 us -> 567 us  [the longest x1 539 us: shards(): pl.pallas_call(functools.partial(regroup, parts, owners), in_specs=[any_s...]
    all_to_all x3 -> x1, waiting for transfers between devices: 405 us -> 0.01 us  [shards(): got = lax.all_to_all(last, 'rows', split_axis=0, concat_axis=0, tiled=True)]
    psum x1 -> x0, waiting for transfers between devices: 61.4 us -> none  [shards(): lax.psum((jnp.concatenate((part_up, part_rest)), part_down), 'rows')]
    all_gather x2 -> x0, blocking collectives: 25.5 us -> none  [the longest x1 16.5 us: shards(): lax.all_gather(jnp.concatenate((head, part_router.reshape(-1, 1, wide))),...]
    all_to_all x3 -> x1, starting transfers between devices: 14.9 us -> 6.36 us  [shards(): got = lax.all_to_all(last, 'rows', split_axis=0, concat_axis=0, tiled=True)]
  transfers between devices with their start and end apart: 4 -> 1, of which waited for: 4 -> 0; matrix products, arithmetic and copies ran while one was open for 1% -> 0% of each run, Pallas kernels for 12% -> 5%
where the time goes in v1:
time: 576 us; the launch traced here: 575 us
  Pallas kernels  567 us (98%)
  starting transfers between devices  6.36 us (1%)
    pallas_call x1, Pallas kernels, shards(): pl.pallas_call(functools.partial(regroup, parts, owners), in_specs=[any_s...  539 us
    pallas_call x4, Pallas kernels, placed(): pl.pallas_call(body, grid=(count // step,), in_specs=specs, out_specs=pl....  27.6 us
  transfers between devices with their start and end apart: 1, of which 0 were waited for; matrix products, arithmetic and copies ran while one was open for 0% of the time, Pallas kernels for 5%

profile of v1, /device:TPU:0, one launch (start us, length us, event | category | flops | bytes accessed | tf_op | source)
XLA Modules:
  0.0 574.9 jit_solution(3049828203730186186)
XLA Ops:
  0.6 538.9 %shard_map.135 = (bf16[16,2048,128]{2,1,0:T(8,128)(2,1)}, bf16[16,2048,128]{2,1,0:T(8,128)(2,1)}, bf16[16,128,2048]{2,1,0:T(8,128)(2,1)}, bf16[8,2,128,256]{3,2,...) custom-call(f32[16,256,1024]{2,1,0:T(8,128)} %wg.1, bf16[16,256,1024]{2,1,0:T(8,128)(2,1)} %ag.1, ...), custom_call_target="tpu_custom_call" | custom-call | flops 1073741824 | bytes 268435456 | tf_op jit(solution)/shard_map/pallas_call | solution.py:316
  539.6 6.4 %all-to-all-start = ((bf16[8,2,128,256]{3,2,1,0:T(8,128)(2,1)}), bf16[8,2,128,256]{3,2,1,0:T(8,128)(2,1)S(1)}, u32[]{:S(2)}, u32[]{:S(2)}) async-start(bf16[8,2,128,256]{3,2,1,0:T(8,128)(2,1)} %get-tuple-element.15), calls=%async_computation | async-start | bytes 2097152 | tf_op jit(solution)/shard_map/all_to_all | solution.py:355
  545.9 8.6 %shard_map.138.refs_0_ = bf16[16,128,2048]{2,1,0:T(8,128)(2,1)} custom-call(bf16[16,128,2048]{2,1,0:T(8,128)(2,1)} %get-tuple-element.16.x), custom_call_target="tpu_custom_call" | custom-call | flops 29360128 | bytes 29360128 | tf_op jit(solution)/shard_map/pallas_call | solution.py:287
  554.6 8.9 %shard_map.136 = bf16[16,2048,128]{2,1,0:T(8,128)(2,1)} custom-call(bf16[16,2048,128]{2,1,0:T(8,128)(2,1)} %get-tuple-element.13.x), custom_call_target="tpu_custom_call" | custom-call | flops 33554432 | bytes 33554432 | tf_op jit(solution)/shard_map/pallas_call | solution.py:287
  563.5 0.0 copy-start.1
  563.5 9.0 %shard_map.137 = bf16[16,2048,128]{2,1,0:T(8,128)(2,1)} custom-call(bf16[16,2048,128]{2,1,0:T(8,128)(2,1)} %get-tuple-element.14.x), custom_call_target="tpu_custom_call" | custom-call | flops 33554432 | bytes 33554432 | tf_op jit(solution)/shard_map/pallas_call | solution.py:287
  572.5 0.0 copy-done.1
  572.5 0.6 fusion
  573.1 0.0 copy-start
  573.1 0.0 all-to-all-done.x
  573.1 1.1 shard_map.139
  574.2 0.0 copy-done
  574.2 0.7 copy.18
Async XLA Ops:
  539.6 33.5 %all-to-all-start = ((bf16[8,2,128,256]{3,2,1,0:T(8,128)(2,1)}), bf16[8,2,128,256]{3,2,1,0:T(8,128)(2,1)S(1)}, u32[]{:S(2)}, u32[]{:S(2)}) async-start(bf16[8,2,128,256]{3,2,1,0:T(8,128)(2,1)} %get-tuple-element.15), calls=%async_computation | async-start | bytes 2097152 | tf_op jit(solution)/shard_map/all_to_all | solution.py:355
  563.5 9.0 %copy-start.1 = (f32[48,1,128]{2,1,0:T(1,128)S(1)}, f32[48,1,128]{2,1,0:T(1,128)}, u32[]{:S(2)}) copy-start(f32[48,1,128]{2,1,0:T(1,128)} %get-tuple-element.17) | copy-start | bytes 73732
  573.1 1.1 copy-start

commit v2 on v1

v2 whole, which is shorter than its diff:
```python
import functools

import jax
import jax.numpy as jnp
from jax import lax
from jax.experimental import pallas as pl
from jax.experimental.pallas import tpu as pltpu
from jax.sharding import PartitionSpec as P

LANES = 128
HEAD = 2
EARLY = 8
RING = 4
TAIL = 2
MESH = pl.DeviceIdType.MESH


def remote(src, dst, send, recv, peer, axis="rows"):
    return pltpu.make_async_remote_copy(
        src_ref=src, dst_ref=dst, send_sem=send, recv_sem=recv, device_id={axis: peer}, device_id_type=MESH
    )


def regroup(
    parts, owners,
    wg, ag, wu, au, wd, ad, rw, gain,
    og, ou, od, ot, oscale, orouter,
    wbuf, abuf, wdbuf, adbuf, sg, su, sd, direct, near, early, early_heard, early_factors,
    rest, rest_heard, factors, scales, rwbuf, gainbuf, piece, router,
    in_sem, down_sem, direct_send, direct_recv, early_send, early_recv, give_send, give_recv, back_send, back_recv,
    data_send, data_recv, kept, piece_send, piece_recv, router_send, router_recv, small,
):
    me = lax.axis_index("rows")
    own = lax.axis_index("owner")
    experts, high = wg.shape[0], wg.shape[1]
    deep = wd.shape[2]
    tail = ot.shape[1]
    levels = parts.bit_length() - 1
    bits = [lax.rem(me // 2**level, 2) for level in range(levels)]

    def peer(k):
        return lax.rem(me + k, parts)

    def mirrored(index):
        return sum(lax.rem(index // 2**i, 2) * 2 ** (levels - 1 - i) for i in range(levels))

    def fetch(w, a, e, wv, av, sem, slot):
        pltpu.make_async_copy(w.at[e], wv.at[slot], sem.at[0, slot]).start()
        pltpu.make_async_copy(a.at[e], av.at[slot], sem.at[1, slot]).start()

    def fetched(w, a, e, wv, av, sem, slot):
        pltpu.make_async_copy(w.at[e], wv.at[slot], sem.at[0, slot]).wait()
        pltpu.make_async_copy(a.at[e], av.at[slot], sem.at[1, slot]).wait()

    def landed(ref, sem):
        pltpu.make_async_copy(ref, ref, sem).wait()

    def stream(w, a, wv, av, sem, base, first, count, body):
        for i in range(min(RING - 1, count)):
            fetch(w, a, first + i, wv, av, sem, base + i)

        @pl.loop(0, count)
        def _(i):
            slot = base + lax.rem(i, RING)
            fetched(w, a, first + i, wv, av, sem, slot)

            @pl.when(i + RING - 1 < count)
            def _():
                fetch(w, a, first + i + RING - 1, wv, av, sem, base + lax.rem(i + RING - 1, RING))

            body(first + i, slot)

    def lanes(p):
        return pl.ds(pl.multiple_of(p * LANES, LANES), LANES)

    def columns_sum(slot, put):
        @pl.loop(0, parts)
        def _(s):
            p = mirrored(s)
            fresh = wbuf[slot, :, lanes(p)] + abuf[slot, :, lanes(p)].astype(jnp.float32)
            put(s, jnp.sum(fresh * fresh, axis=0, keepdims=True))

    def rows_sum(slot, put):
        @pl.loop(0, parts)
        def _(s):
            p = mirrored(s)
            fresh = wdbuf[slot, lanes(p), :] + adbuf[slot, lanes(p), :].astype(jnp.float32)
            square = fresh * fresh
            folded = square[:, :LANES]
            for start in range(LANES, deep, LANES):
                folded = folded + square[:, start : start + LANES]
            put(s, jnp.sum(folded.T, axis=0, keepdims=True))

    def columns_norm(take, e, slot, send):
        @pl.loop(0, parts)
        def _(s):
            p = mirrored(s)
            fresh = wbuf[slot, :, lanes(p)] + abuf[slot, :, lanes(p)].astype(jnp.float32)
            send[e, p] = (fresh * take(s)).astype(send.dtype)

    def rows_norm(take, e, slot):
        @pl.loop(0, parts)
        def _(s):
            p = mirrored(s)
            factor = jnp.broadcast_to(take(s), (LANES, LANES)).T
            for start in range(0, deep, LANES):
                fresh = wdbuf[slot, lanes(p), start : start + LANES]
                fresh = fresh + adbuf[slot, lanes(p), start : start + LANES].astype(jnp.float32)
                sd[e, p, :, start : start + LANES] = (fresh * factor).astype(sd.dtype)

    def put_head(unit):
        def put(s, row):
            direct[me, unit, pl.ds(s, 1), :] = row
            early[s, pl.ds(unit, 1), :] = row

        return put

    def put_in(ref, row):
        def put(s, value):
            ref[s, pl.ds(row, 1), :] = value

        return put

    def taken(ref, row):
        return lambda s: ref[s, pl.ds(row, 1), :]

    def push(kind, e):
        send, stage = ((sg, og), (su, ou), (sd, od))[kind]
        if kind < 2:
            place = stage.at[e, pl.ds(pl.multiple_of(me * high, high), high), :]
        else:
            place = stage.at[e, :, pl.ds(pl.multiple_of(me * deep, deep), deep)]

        @pl.loop(1, parts)
        def _(k):
            remote(send.at[e, peer(k)], place, data_send.at[kind], data_recv.at[kind], peer(k)).start()

        pltpu.make_async_copy(send.at[e, me], place, kept.at[kind]).start()

    def span(level):
        half = parts >> (level + 1)
        start = sum(bits[i] * (parts >> (i + 1)) for i in range(level))
        return start + bits[level] * half, start + (1 - bits[level]) * half, half, me + (1 - 2 * bits[level]) * 2**level

    def heard(level):
        return rest_heard.at[pl.ds(parts - (parts >> level), parts >> (level + 1))]

    def give(level):
        _, away, half, partner = span(level)
        remote(rest.at[pl.ds(away, half)], heard(level), give_send.at[level], give_recv.at[level], partner).start()

    def gain_level(level):
        keep, _, half, _ = span(level)
        landed(heard(level), give_recv.at[level])
        first = parts - (parts >> level)
        for i in range(half):
            rest[keep + i] = rest[keep + i] + rest_heard[first + i]

    def back(level):
        keep, _, half, partner = span(level)
        mine = factors.at[pl.ds(keep, half)]
        remote(mine, mine, back_send.at[level], back_recv.at[level], partner).start()

    def regain(level):
        half = parts >> (level + 1)
        landed(factors.at[pl.ds(0, half)], back_recv.at[level])

    barrier = pltpu.get_barrier_semaphore()
    fetch(wg, ag, 0, wbuf, abuf, in_sem, 0)
    fetch(wg, ag, 1, wbuf, abuf, in_sem, 1)
    pltpu.make_async_copy(rw, rwbuf, small.at[0]).start()
    pltpu.make_async_copy(gain, gainbuf, small.at[1]).start()

    @pl.loop(1, parts)
    def _(k):
        pl.semaphore_signal(barrier, inc=1, device_id={"rows": peer(k)}, device_id_type=MESH)

    for k in range(1, owners):
        pl.semaphore_signal(barrier, inc=1, device_id={"owner": lax.rem(own + k, owners)}, device_id_type=MESH)

    for unit in range(HEAD):
        fetched(wg, ag, unit, wbuf, abuf, in_sem, unit)
        for later in range(2 * unit + HEAD, 2 * unit + HEAD + 2):
            fetch(wg, ag, later, wbuf, abuf, in_sem, later)
        columns_sum(unit, put_head(unit))

    landed(rwbuf, small.at[0])
    landed(gainbuf, small.at[1])
    piece[...] = (rwbuf[...] * gainbuf[...]).astype(piece.dtype)
    pl.semaphore_wait(barrier, parts - 1 + owners - 1)

    @pl.loop(1, parts)
    def _(k):
        remote(direct.at[me], direct.at[me], direct_send, direct_recv, peer(k)).start()

    for later in range(3 * HEAD, EARLY):
        fetch(wg, ag, later, wbuf, abuf, in_sem, later)
    strip = router.at[own, :, pl.ds(pl.multiple_of(me * high, high), high)]

    @pl.loop(1, parts)
    def _(k):
        remote(piece, strip, piece_send, piece_recv, peer(k)).start()

    @pl.loop(HEAD, EARLY)
    def _(unit):
        fetched(wg, ag, unit, wbuf, abuf, in_sem, unit)
        columns_sum(unit, put_in(early, unit))

    landed(direct.at[pl.ds(0, parts - 1)], direct_recv)
    total = direct[0]
    for source in range(1, parts):
        total = total + direct[source]
    near[...] = 1.0 / jnp.sqrt(total)
    columns_norm(lambda s: near[0, pl.ds(s, 1), :], 0, 0, sg)

    @pl.loop(1, parts)
    def _(k):
        remote(early.at[mirrored(peer(k))], early_heard.at[me], early_send.at[0], early_recv.at[0], peer(k)).start()

    push(0, 0)
    columns_norm(lambda s: near[1, pl.ds(s, 1), :], 1, 1, sg)
    landed(early_heard.at[pl.ds(0, parts - 1)], early_recv.at[0])
    mine = mirrored(me)
    total = early[mine]
    for k in range(1, parts):
        total = total + early_heard[peer(k)]
    scale = jnp.sqrt(total)
    scales[0:EARLY] = scale
    early_factors[mine] = 1.0 / scale

    @pl.loop(1, parts)
    def _(k):
        ref = early_factors.at[mine]
        remote(ref, ref, early_send.at[1], early_recv.at[1], peer(k)).start()

    router[own, :, pl.ds(pl.multiple_of(me * high, high), high)] = piece[...]
    push(0, 1)

    first_up, first_down = experts - EARLY, 2 * experts - EARLY
    stream(
        wg, ag, wbuf, abuf, in_sem, EARLY, EARLY, experts - EARLY,
        lambda e, slot: columns_sum(slot, put_in(rest, e - EARLY)),
    )
    stream(
        wu, au, wbuf, abuf, in_sem, EARLY, 0, experts,
        lambda e, slot: columns_sum(slot, put_in(rest, first_up + e)),
    )
    landed(early_factors.at[pl.ds(0, parts - 1)], early_recv.at[1])

    @pl.loop(HEAD, EARLY)
    def _(unit):
        columns_norm(taken(early_factors, unit), unit, unit, sg)

    push(0, HEAD)
    push(0, HEAD + 1)
    stream(
        wd, ad, wdbuf, adbuf, down_sem, 0, 0, experts,
        lambda e, slot: rows_sum(slot, put_in(rest, first_down + e)),
    )
    give(0)
    gain_level(0)
    sent = HEAD + 2
    for level in range(1, levels):
        give(level)
        push(0, sent)
        sent += 1
        gain_level(level)
    keep = span(levels - 1)[0]
    scale = jnp.sqrt(rest[keep])
    scales[EARLY:] = scale
    factors[keep] = 1.0 / scale
    pltpu.make_async_copy(scales, oscale, small.at[0]).start()
    for level in range(levels - 1, 0, -1):
        back(level)
        push(0, sent)
        sent += 1
        regain(level)
    for left in range(sent, EARLY):
        push(0, left)
    back(0)
    regain(0)

    def gate(e, slot):
        columns_norm(taken(factors, e - EARLY), e, slot, sg)

        @pl.when(e > EARLY)
        def _():
            push(0, e - 1)

    def up(e, slot):
        columns_norm(taken(factors, first_up + e), e, slot, su)

        @pl.when(e > 0)
        def _():
            push(1, e - 1)

    def down(e, slot):
        rows_norm(taken(factors, first_down + e), e, slot)

        @pl.when((e > 0) & (e <= experts - tail))
        def _():
            push(2, e - 1)

    stream(wg, ag, wbuf, abuf, in_sem, EARLY, EARLY, experts - EARLY, gate)
    push(0, experts - 1)

    gathered = router.at[own, :, pl.ds(0, (parts - 1) * high)]
    landed(gathered, piece_recv)
    for k in range(1, owners):
        remote(
            router.at[own], router.at[own], router_send, router_recv, lax.rem(own + k, owners), "owner"
        ).start()

    stream(wu, au, wbuf, abuf, in_sem, EARLY, 0, experts, up)
    push(1, experts - 1)
    stream(wd, ad, wdbuf, adbuf, down_sem, 0, 0, experts, down)

    for i in range(tail):
        pltpu.make_async_copy(sd.at[experts - tail + i], ot.at[:, i], kept.at[3]).start()

    arrived = router.at[pl.ds(0, owners - 1)]
    landed(arrived, router_recv)
    pltpu.make_async_copy(router, orouter, small.at[1]).start()

    landed(direct.at[pl.ds(0, parts - 1)], direct_send)
    landed(early.at[pl.ds(0, parts - 1)], early_send.at[0])
    landed(early.at[pl.ds(0, parts - 1)], early_send.at[1])
    for level in range(levels):
        half = rest.at[pl.ds(0, parts >> (level + 1))]
        landed(half, give_send.at[level])
        landed(half, back_send.at[level])
    landed(gathered, piece_send)
    landed(arrived, router_send)
    pltpu.make_async_copy(scales, oscale, small.at[0]).wait()
    pltpu.make_async_copy(router, orouter, small.at[1]).wait()
    landed(sd.at[pl.ds(experts - tail, tail)], kept.at[3])
    for kind, send in enumerate((sg, su, sd)):
        count = experts - tail if kind == 2 else experts
        landed(send.at[pl.ds(0, count), 0], kept.at[kind])
        most = send.at[pl.ds(0, count), pl.ds(0, parts - 1)]
        landed(most, data_send.at[kind])
        landed(most, data_recv.at[kind])


def publish(depth, sg, su, sd, scale, router, og, ou, od, o1, o2, o3, orouter, tall, flat, sbuf, rbuf, load, store, small):
    slots = tall.shape[0]
    experts = og.shape[0]
    jobs = [(stage, out, tall, e) for stage, out in ((sg, og), (su, ou)) for e in range(experts)]
    jobs += [(sd, od, flat, e) for e in range(od.shape[0] - TAIL)]

    def read(i):
        stage, _, buffer, e = jobs[i]
        return pltpu.make_async_copy(stage.at[e], buffer.at[i % slots], load.at[i % slots])

    def write(i):
        _, out, buffer, e = jobs[i]
        return pltpu.make_async_copy(buffer.at[i % slots], out.at[e], store.at[i % slots])

    extras = [pltpu.make_async_copy(scale, sbuf, small.at[0]), pltpu.make_async_copy(router, rbuf, small.at[1])]
    for copy in extras:
        copy.start()
    for i in range(len(jobs) + depth):
        if i < len(jobs):
            if i >= slots:
                write(i - slots).wait()
            read(i).start()
        if i >= depth:
            read(i - depth).wait()
            write(i - depth).start()
    for copy in extras:
        copy.wait()
    outs = [pltpu.make_async_copy(sbuf.at[pl.ds(i * experts, experts)], o, small.at[2 + i]) for i, o in enumerate((o1, o2, o3))]
    columns = rbuf.shape[1]
    for i in range(rbuf.shape[0]):
        outs.append(pltpu.make_async_copy(rbuf.at[i], orouter.at[pl.ds(i * columns, columns)], small.at[5 + i]))
    for copy in outs:
        copy.start()
    for i in range(max(0, len(jobs) - slots), len(jobs)):
        write(i).wait()
    for copy in outs:
        copy.wait()


def stack_columns(x, *refs):
    o = refs[-1]
    deep = x.shape[2]
    for source in range(x.shape[0]):
        o[:, source * deep : (source + 1) * deep] = x[source]


def shards(parts, owners, w_gate, avg_gate, w_up, avg_up, w_down, avg_down, router_weight, router_gain):
    experts, high, wide = w_gate.shape
    tall, deep = w_down.shape[1:]
    block, slab = wide // parts, tall // parts
    units, slots, later = 3 * experts, EARLY + RING, 3 * experts - EARLY
    columns, model = router_weight.shape[1], parts * high
    levels = parts.bit_length() - 1
    f32, bf16 = jnp.float32, jnp.bfloat16
    any_spec = pl.BlockSpec(memory_space=pl.ANY)
    shape_columns, shape_down = (experts, high * parts, block), (experts, slab, deep * parts)
    dma = pltpu.SemaphoreType.DMA

    *stages, last, scales, routers = pl.pallas_call(
        functools.partial(regroup, parts, owners),
        in_specs=[any_spec] * 8,
        out_specs=[any_spec] * 6,
        out_shape=[
            jax.ShapeDtypeStruct(shape_columns, bf16),
            jax.ShapeDtypeStruct(shape_columns, bf16),
            jax.ShapeDtypeStruct(shape_down, bf16),
            jax.ShapeDtypeStruct((parts, TAIL, slab, deep), bf16),
            jax.ShapeDtypeStruct((units, LANES), f32),
            jax.ShapeDtypeStruct((owners, columns, model), bf16),
        ],
        scratch_shapes=[
            pltpu.VMEM((slots, high, wide), f32),
            pltpu.VMEM((slots, high, wide), bf16),
            pltpu.VMEM((RING, tall, deep), f32),
            pltpu.VMEM((RING, tall, deep), bf16),
            pltpu.VMEM((experts, parts, high, block), bf16),
            pltpu.VMEM((experts, parts, high, block), bf16),
            pltpu.VMEM((experts, parts, slab, deep), bf16),
            pltpu.VMEM((parts, HEAD, parts, LANES), f32),
            pltpu.VMEM((HEAD, parts, LANES), f32),
            pltpu.VMEM((parts, EARLY, LANES), f32),
            pltpu.VMEM((parts, EARLY, LANES), f32),
            pltpu.VMEM((parts, EARLY, LANES), f32),
            pltpu.VMEM((parts, later, LANES), f32),
            pltpu.VMEM((parts - 1, later, LANES), f32),
            pltpu.VMEM((parts, later, LANES), f32),
            pltpu.VMEM((units, LANES), f32),
            pltpu.VMEM((columns, high), f32),
            pltpu.VMEM((1, high), f32),
            pltpu.VMEM((columns, high), bf16),
            pltpu.VMEM((owners, columns, model), bf16),
            dma((2, slots)), dma((2, RING)), dma, dma, dma((2,)), dma((2,)),
            dma((levels,)), dma((levels,)), dma((levels,)), dma((levels,)),
            dma((3,)), dma((3,)), dma((4,)), dma, dma, dma, dma, dma((2,)),
        ],
        cost_estimate=pl.CostEstimate(flops=2**30, bytes_accessed=2**28, transcendentals=0),
        compiler_params=pltpu.CompilerParams(
            collective_id=0, has_side_effects=True, vmem_limit_bytes=60 * 2**20
        ),
    )(w_gate, avg_gate, w_up, avg_up, w_down, avg_down, router_weight.T, router_gain.reshape(1, high))

    got = lax.all_to_all(last, "rows", split_axis=0, concat_axis=0, tiled=True)
    serve_gate, serve_up, held, scale_gate, scale_up, scale_down, serve_router = pl.pallas_call(
        functools.partial(publish, 8),
        in_specs=[any_spec] * 5,
        out_specs=[any_spec] * 7,
        out_shape=[
            jax.ShapeDtypeStruct(shape_columns, bf16),
            jax.ShapeDtypeStruct(shape_columns, bf16),
            jax.ShapeDtypeStruct(shape_down, bf16),
            *[jax.ShapeDtypeStruct((experts, LANES), f32)] * 3,
            jax.ShapeDtypeStruct((owners * columns, model), bf16),
        ],
        scratch_shapes=[
            pltpu.VMEM((16,) + shape_columns[1:], bf16),
            pltpu.VMEM((16,) + shape_down[1:], bf16),
            pltpu.VMEM((units, LANES), f32),
            pltpu.VMEM((owners, columns, model), bf16),
            dma((16,)), dma((16,)), dma((5 + owners,)),
        ],
        cost_estimate=pl.CostEstimate(flops=2**26, bytes_accessed=2**26, transcendentals=0),
        compiler_params=pltpu.CompilerParams(vmem_limit_bytes=40 * 2**20),
    )(*stages, scales, routers)
    serve_down = pl.pallas_call(
        stack_columns,
        grid=(TAIL,),
        in_specs=[pl.BlockSpec((parts, None, slab, deep), lambda e: (0, e, 0, 0)), any_spec],
        out_specs=pl.BlockSpec((None,) + shape_down[1:], lambda e: (experts - TAIL + e, 0, 0)),
        out_shape=jax.ShapeDtypeStruct(shape_down, bf16),
        input_output_aliases={1: 0},
        cost_estimate=pl.CostEstimate(flops=2**21, bytes_accessed=2**22, transcendentals=0),
        compiler_params=pltpu.CompilerParams(vmem_limit_bytes=16 * 2**20),
    )(got, held)
    return (serve_gate, serve_up, serve_down, scale_gate, scale_up, scale_down, serve_router.T)


def plain_shards(w_gate, avg_gate, w_up, avg_up, w_down, avg_down, router_weight, router_gain):
    def served(w, a, axis, split):
        fresh = w + a.astype(jnp.float32)
        scale = jnp.sqrt(lax.psum(jnp.sum(fresh * fresh, axis=axis), "rows"))
        narrow = (fresh / jnp.expand_dims(scale, axis)).astype(jnp.bfloat16)
        serve = lax.all_to_all(narrow, "rows", split_axis=split, concat_axis=axis, tiled=True)
        width = serve.shape[split]
        return serve, lax.dynamic_slice_in_dim(scale, lax.axis_index("rows") * width, width, axis=1)

    serve_gate, scale_gate = served(w_gate, avg_gate, 1, 2)
    serve_up, scale_up = served(w_up, avg_up, 1, 2)
    serve_down, scale_down = served(w_down, avg_down, 2, 1)
    part_router = (router_weight * router_gain[:, None]).astype(jnp.bfloat16)
    row_router = lax.all_gather(part_router, "rows", axis=0, tiled=True)
    serve_router = lax.all_gather(row_router, "owner", axis=1, tiled=True)
    return (serve_gate, serve_up, serve_down, scale_gate, scale_up, scale_down, serve_router)


def solution(mesh):
    parts, owners = mesh.shape["rows"], mesh.shape["owner"]

    def dispatched(*args):
        experts, high, wide = args[0].shape
        tall, deep = args[4].shape[1:]
        block, slab = wide // parts, tall // parts
        columns = args[6].shape[1]
        aligned = block == LANES and slab == LANES and deep % LANES == 0 and high % LANES == 0
        aligned = aligned and high <= 256 and deep <= 256 and experts <= 16 and experts % 8 == 0
        aligned = aligned and experts > EARLY and columns % 16 == 0 and parts == 8 and owners > 1
        return shards(parts, owners, *args) if aligned else plain_shards(*args)

    return jax.shard_map(
        dispatched,
        mesh=mesh,
        in_specs=(
            P("owner", "rows", None),
            P("owner", "rows", None),
            P("owner", "rows", None),
            P("owner", "rows", None),
            P("owner", None, "rows"),
            P("owner", None, "rows"),
            P("rows", "owner"),
            P("rows"),
        ),
        out_specs=(
            P("owner", None, "rows"),
            P("owner", None, "rows"),
            P("owner", "rows", None),
            P("owner", "rows"),
            P("owner", "rows"),
            P("owner", "rows"),
            P(),
        ),
        check_vma=False,
    )
```

time: 576 us -> 564 us (0.979)
  Pallas kernels: 567 us -> 545 us
  waiting for transfers between devices: 0.01 us -> 6.7 us
    pallas_call x4 -> x2, Pallas kernels: 27.6 us -> 15.9 us  [the longest x1 14.8 us: shards(): pl.pallas_call(functools.partial(publish, 8), in_specs=[any_spec] * 5, ou...]
    pallas_call x1, Pallas kernels: 539 us -> 529 us  [shards(): pl.pallas_call(functools.partial(regroup, parts, owners), in_specs=[any_s...]
    all_to_all x1, waiting for transfers between devices: 0.01 us -> 6.7 us  [shards(): got = lax.all_to_all(last, 'rows', split_axis=0, concat_axis=0, tiled=True)]
  transfers between devices with their start and end apart: 1 -> 1, of which waited for: 0 -> 1; matrix products, arithmetic and copies ran while one was open for 0% -> 0% of each run, Pallas kernels for 5% -> 3%
where the time goes in v2:
time: 564 us
  Pallas kernels  545 us (97%)
  waiting for transfers between devices  6.7 us (1%)
  starting transfers between devices  6.58 us (1%)
    pallas_call x1, Pallas kernels, shards(): pl.pallas_call(functools.partial(regroup, parts, owners), in_specs=[any_s...  529 us
    pallas_call x1, Pallas kernels, shards(): pl.pallas_call(functools.partial(publish, 8), in_specs=[any_spec] * 5, ou...  14.8 us
  transfers between devices with their start and end apart: 1, of which 1 were waited for; matrix products, arithmetic and copies ran while one was open for 0% of the time, Pallas kernels for 3%

profile of v2, /device:TPU:0, one launch (start us, length us, event | category | flops | bytes accessed | tf_op | source)
XLA Modules:
  0.0 563.7 jit_solution(11144099236274963347)
XLA Ops:
  0.6 528.8 %shard_map.135 = (bf16[16,2048,128]{2,1,0:T(8,128)(2,1)}, bf16[16,2048,128]{2,1,0:T(8,128)(2,1)}, bf16[16,128,2048]{2,1,0:T(8,128)(2,1)}, bf16[8,2,128,256]{3,2,...) custom-call(f32[16,256,1024]{2,1,0:T(8,128)} %wg.1, bf16[16,256,1024]{2,1,0:T(8,128)(2,1)} %ag.1, ...), custom_call_target="tpu_custom_call" | custom-call | flops 1073741824 | bytes 268435456 | tf_op jit(solution)/shard_map/pallas_call | solution.py:403
  529.5 6.6 %all-to-all-start = ((bf16[8,2,128,256]{3,2,1,0:T(8,128)(2,1)}), bf16[8,2,128,256]{3,2,1,0:T(8,128)(2,1)S(1)}, u32[]{:S(2)}, u32[]{:S(2)}) async-start(bf16[8,2,128,256]{3,2,1,0:T(8,128)(2,1)} %get-tuple-element.27), calls=%async_computation | async-start | bytes 2097152 | tf_op jit(solution)/shard_map/all_to_all | solution.py:446
  536.0 0.0 copy-start
  536.0 3.4 copy-done
  539.4 0.0 copy-start.1
  539.4 0.9 copy-done.1
  540.4 0.0 copy-start.2
  540.4 0.7 copy-done.2
  541.1 14.8 %shard_map.136 = (bf16[16,2048,128]{2,1,0:T(8,128)(2,1)}, bf16[16,2048,128]{2,1,0:T(8,128)(2,1)}, bf16[16,128,2048]{2,1,0:T(8,128)(2,1)}, f32[16,128]{1,0:T(8,12...) custom-call(bf16[16,2048,128]{2,1,0:T(8,128)(2,1)S(1)} %copy-done, ...), custom_call_target="tpu_custom_call" | custom-call | flops 67108864 | bytes 67108864 | tf_op jit(solution)/shard_map/pallas_call | solution.py:447
  555.9 6.7 %all-to-all-done.x = bf16[8,2,128,256]{3,2,1,0:T(8,128)(2,1)S(1)} async-done(((bf16[8,2,128,256]{3,2,1,0:T(8,128)(2,1)}), bf16[8,2,128,256]{3,2,1,0:T(8,128)(2,1)S(1)}, u32[]{:S(2)}, u32[]{:S(2)}) %all-to-all-start) | async-done | bytes 1048608 | tf_op jit(solution)/shard_map/all_to_all | solution.py:446
  562.6 1.1 shard_map.137
Async XLA Ops:
  529.5 33.1 %all-to-all-start = ((bf16[8,2,128,256]{3,2,1,0:T(8,128)(2,1)}), bf16[8,2,128,256]{3,2,1,0:T(8,128)(2,1)S(1)}, u32[]{:S(2)}, u32[]{:S(2)}) async-start(bf16[8,2,128,256]{3,2,1,0:T(8,128)(2,1)} %get-tuple-element.27), calls=%async_computation | async-start | bytes 2097152 | tf_op jit(solution)/shard_map/all_to_all | solution.py:446
  536.0 3.4 copy-start
  539.4 0.9 copy-start.1
  540.4 0.7 copy-start.2
